TPU v7x, 32 devices: a whole 2x2x4 slice. The times are simulated.
32 devices in a mesh: row: 8 (over z, core), col: 4 (over y, x).
Axes of the slice: x: 2, y: 2, z: 4, core: 2. Of those that a mesh axis runs over, the one named last changes fastest.
Arguments:
- tokens: bfloat16 [12288, 2048], P('row', 'col'), may hold values from -6 to 6
- weight_query: bfloat16 [2048, 2048], P('row', 'col'), may hold values from -0.125 to 0.125
- weight_key: bfloat16 [2048, 2048], P('row', 'col'), may hold values from -0.125 to 0.125
- weight_value: bfloat16 [2048, 2048], P('row', 'col'), may hold values from -0.125 to 0.125
- weight_output: bfloat16 [2048, 2048], P('col', 'row'), may hold values from -0.125 to 0.125
- weight_gate: bfloat16 [2048, 8192], P('row', 'col'), may hold values from -0.125 to 0.125
- weight_up: bfloat16 [2048, 8192], P('row', 'col'), may hold values from -0.125 to 0.125
- weight_down: bfloat16 [8192, 2048], P('col', 'row'), may hold values from -0.0625 to 0.0625
- gain_query: float32 [2048], P('col'), may hold values from 0.25 to 1.75
- gain_key: float32 [2048], P('col'), may hold values from 0.25 to 1.75
- gain_attention: float32 [2048], replicated, may hold values from 0.5 to 1.5
- gain_feedforward: float32 [2048], replicated, may hold values from 0.5 to 1.5
- positions: int32 [12288], P('row'), may hold values from 0 to 1279, as said below
- segments: int32 [12288], P('row'), may hold values from 0 to 2, as said below
- cotangent: bfloat16 [12288, 2048], P('row', 'col'), may hold values from -6 to 6
Outputs:
- activations: bfloat16 [12288, 2048], P('row', 'col')
- input_grad: float32 [12288, 2048], P('row', 'col')
- query_weight_grad: float32 [2048, 2048], P('row', 'col')
- key_weight_grad: float32 [2048, 2048], P('row', 'col')
- value_weight_grad: float32 [2048, 2048], P('row', 'col')
- output_weight_grad: float32 [2048, 2048], P('col', 'row')
- gate_weight_grad: float32 [2048, 8192], P('row', 'col')
- up_weight_grad: float32 [2048, 8192], P('row', 'col')
- down_weight_grad: float32 [8192, 2048], P('col', 'row')
- query_gain_grad: float32 [2048], P('col')
- key_gain_grad: float32 [2048], P('col')
- attention_gain_grad: float32 [2048], replicated
- feedforward_gain_grad: float32 [2048], replicated
Inputs may be any that keep to these rules, and one draw needn't show every extreme that they name: The 1536 rows of each index of row form one group: the prompt's 1024 rows are consecutive with segment 0 and positions 0 to 1023; each continuation has 256 consecutive rows, one segment of 1 to 2 (each once a group) and positions 1024 to 1279 in order; the prompt lies before, between or after whole continuations. `segments`: segment ids of the layout described for positions.
All inputs are finite; a program needn't handle non-finite values.
Results may differ from a plain program's by a relative error of at most 0.02.
Values may be sent and summed in bfloat16 or wider, within the bound.
A program may use at most 320 MiB of HBM per device.

v0:
```python
import jax
import jax.numpy as jnp
from jax import lax
from jax.sharding import PartitionSpec as P

D = 2048
HD = 128
EPSILON = 1e-06
ROPE_BASE = 500000.0
NEGATIVE = -1e30
block_limit = 512


def times_plain(left, right):
    return jnp.dot(left, right, preferred_element_type=jnp.float32)


def times_transposed(left, right):
    return lax.dot_general(
        left, right, (((1,), (1,)), ((), ())), preferred_element_type=jnp.float32
    )


def transposed_times(left, right):
    return lax.dot_general(
        left, right, (((0,), (0,)), ((), ())), preferred_element_type=jnp.float32
    )


def rotation(positions):
    half_dim = HD // 2
    inverse = ROPE_BASE ** (-(jnp.arange(half_dim).astype(jnp.float32) * 2.0) / HD)
    angles = positions.astype(jnp.float32)[:, None] * inverse[None, :]
    return (jnp.cos(angles), jnp.sin(angles))


def rotate(values, cosine_table, sine_table, direction):
    row_count, local_width = values.shape
    local_heads = local_width // HD
    half_dim = HD // 2
    shaped = values.reshape(row_count, local_heads, HD)
    lower_half = shaped[..., :half_dim]
    upper_half = shaped[..., half_dim:]
    cosine_rows = cosine_table[:, None, :]
    sine_rows = direction * sine_table[:, None, :]
    rotated = jnp.concatenate(
        [
            lower_half * cosine_rows - upper_half * sine_rows,
            upper_half * cosine_rows + lower_half * sine_rows,
        ],
        axis=-1,
    )
    return rotated.reshape(row_count, local_width)


def allowed_pairs(segment_block, position_block, segments, positions):
    shared = (segments[None, :] == 0) | (segments[None, :] == segment_block[:, None])
    return shared & (positions[None, :] <= position_block[:, None])


def norm_back(incoming, values, norm_scale, gain_vector):
    scaled = gain_vector * incoming
    inner_mean = jnp.mean(scaled * values, axis=-1, keepdims=True)
    grad_values = norm_scale * scaled - values * norm_scale * norm_scale * norm_scale * inner_mean
    return (grad_values, jnp.sum(incoming * values * norm_scale, axis=0))


def spread_share(values, start):
    return lax.dynamic_update_slice_in_dim(jnp.zeros((D,), jnp.float32), values, start, 0)


def attend(query_rot, key_rot, value_low, segments, positions):
    row_count, local_width = query_rot.shape
    local_heads = local_width // HD
    block_rows = min(block_limit, row_count)
    blocks = row_count // block_rows
    key_heads = key_rot.reshape(row_count, local_heads, HD)
    value_heads = value_low.reshape(row_count, local_heads, HD)

    def one_block(packed):
        query_block, segment_block, position_block = packed
        query_heads = query_block.reshape(block_rows, local_heads, HD)
        scores = jnp.einsum(
            "qhd,khd->hqk", query_heads, key_heads, preferred_element_type=jnp.float32
        ) * HD ** (-0.5)
        allowed = allowed_pairs(segment_block, position_block, segments, positions)
        scores = jnp.where(allowed[None], scores, NEGATIVE)
        row_max = jnp.max(scores, axis=-1, keepdims=True)
        exponent = jnp.exp(scores - row_max)
        row_total = jnp.sum(exponent, axis=-1, keepdims=True)
        attn_probs = exponent / row_total
        context = jnp.einsum(
            "hqk,khd->qhd",
            attn_probs.astype(jnp.bfloat16),
            value_heads,
            preferred_element_type=jnp.float32,
        )
        return (context.reshape(block_rows, local_width), (row_max + jnp.log(row_total))[..., 0])

    context, log_norm = lax.map(
        one_block,
        (
            query_rot.reshape(blocks, block_rows, local_width),
            segments.reshape(blocks, block_rows),
            positions.reshape(blocks, block_rows),
        ),
    )
    return (context.reshape(row_count, local_width), log_norm)


def attend_back(query_rot, key_rot, value_low, context_grad, log_norm, segments, positions):
    row_count, local_width = query_rot.shape
    local_heads = local_width // HD
    block_rows = min(block_limit, row_count)
    blocks = row_count // block_rows
    scale_factor = HD ** (-0.5)
    key_heads = key_rot.reshape(row_count, local_heads, HD)
    value_heads = value_low.reshape(row_count, local_heads, HD)

    def one_block(carry, packed):
        key_total, value_total = carry
        query_block, grad_block, norm_block, segment_block, position_block = packed
        query_heads = query_block.reshape(block_rows, local_heads, HD)
        grad_heads = grad_block.reshape(block_rows, local_heads, HD)
        scores = (
            jnp.einsum("qhd,khd->hqk", query_heads, key_heads, preferred_element_type=jnp.float32)
            * scale_factor
        )
        allowed = allowed_pairs(segment_block, position_block, segments, positions)
        scores = jnp.where(allowed[None], scores, NEGATIVE)
        attn_probs = jnp.exp(scores - norm_block[..., None])
        prob_grad = jnp.einsum(
            "qhd,khd->hqk", grad_heads, value_heads, preferred_element_type=jnp.float32
        )
        delta_sum = jnp.sum(attn_probs * prob_grad, axis=-1, keepdims=True)
        score_grad = (attn_probs * (prob_grad - delta_sum)).astype(jnp.bfloat16)
        query_grad = (
            jnp.einsum("hqk,khd->qhd", score_grad, key_heads, preferred_element_type=jnp.float32)
            * scale_factor
        )
        key_total = (
            key_total
            + jnp.einsum(
                "hqk,qhd->khd", score_grad, query_heads, preferred_element_type=jnp.float32
            )
            * scale_factor
        )
        value_total = value_total + jnp.einsum(
            "hqk,qhd->khd",
            attn_probs.astype(jnp.bfloat16),
            grad_heads,
            preferred_element_type=jnp.float32,
        )
        return ((key_total, value_total), query_grad.reshape(block_rows, local_width))

    zeros_heads = jnp.zeros((row_count, local_heads, HD), jnp.float32)
    packed = (
        query_rot.reshape(blocks, block_rows, local_width),
        context_grad.reshape(blocks, block_rows, local_width),
        log_norm,
        segments.reshape(blocks, block_rows),
        positions.reshape(blocks, block_rows),
    )
    (key_grad, value_grad), query_grad = lax.scan(one_block, (zeros_heads, zeros_heads), packed)
    return (
        query_grad.reshape(row_count, local_width),
        key_grad.reshape(row_count, local_width),
        value_grad.reshape(row_count, local_width),
    )


def body(
    tokens,
    weight_query,
    weight_key,
    weight_value,
    weight_output,
    weight_gate,
    weight_up,
    weight_down,
    gain_query,
    gain_key,
    gain_attention,
    gain_feedforward,
    positions,
    segments,
    cotangent,
):
    col_width = tokens.shape[1]
    col_start = lax.axis_index("col") * col_width
    features = lax.all_gather(tokens, "col", axis=1, tiled=True)
    query_matrix, key_matrix, value_matrix, output_matrix, gate_matrix, up_matrix, down_matrix = (
        lax.all_gather(weight_query, "row", axis=0, tiled=True),
        lax.all_gather(weight_key, "row", axis=0, tiled=True),
        lax.all_gather(weight_value, "row", axis=0, tiled=True),
        lax.all_gather(weight_output, "row", axis=1, tiled=True),
        lax.all_gather(weight_gate, "row", axis=0, tiled=True),
        lax.all_gather(weight_up, "row", axis=0, tiled=True),
        lax.all_gather(weight_down, "row", axis=1, tiled=True),
    )
    query_raw = times_plain(features, query_matrix)
    key_raw = times_plain(features, key_matrix)
    value_low = times_plain(features, value_matrix).astype(jnp.bfloat16)
    square_sums = lax.psum(
        (jnp.sum(query_raw * query_raw, axis=-1), jnp.sum(key_raw * key_raw, axis=-1)), "col"
    )
    query_scale = lax.rsqrt(square_sums[0] / D + EPSILON)[:, None]
    key_scale = lax.rsqrt(square_sums[1] / D + EPSILON)[:, None]
    cosine_table, sine_table = rotation(positions)
    query_rot = rotate(query_raw * query_scale * gain_query, cosine_table, sine_table, 1.0).astype(
        jnp.bfloat16
    )
    key_rot = rotate(key_raw * key_scale * gain_key, cosine_table, sine_table, 1.0).astype(
        jnp.bfloat16
    )
    context, log_norm = attend(query_rot, key_rot, value_low, segments, positions)
    context_low = context.astype(jnp.bfloat16)
    attention_part = times_plain(context_low, output_matrix)
    attention_out = lax.psum(attention_part, "col")
    attention_scale = lax.rsqrt(
        jnp.mean(attention_out * attention_out, axis=-1, keepdims=True) + EPSILON
    )
    hidden_state = features.astype(jnp.float32) + attention_out * attention_scale * gain_attention
    hidden_low = hidden_state.astype(jnp.bfloat16)
    gate = times_plain(hidden_low, gate_matrix)
    up_rows = times_plain(hidden_low, up_matrix)
    sigmoid_gate = jax.nn.sigmoid(gate)
    silu_gate = gate * sigmoid_gate
    activated = (silu_gate * up_rows).astype(jnp.bfloat16)
    feedforward_part = times_plain(activated, down_matrix)
    feedforward_out = lax.psum(feedforward_part, "col")
    feedforward_scale = lax.rsqrt(
        jnp.mean(feedforward_out * feedforward_out, axis=-1, keepdims=True) + EPSILON
    )
    result = hidden_state + feedforward_out * feedforward_scale * gain_feedforward
    activations = lax.dynamic_slice_in_dim(result, col_start, col_width, 1).astype(jnp.bfloat16)
    upstream = lax.all_gather(cotangent, "col", axis=1, tiled=True).astype(jnp.float32)
    feedforward_full_grad, feedforward_gain_full = norm_back(
        upstream, feedforward_out, feedforward_scale, gain_feedforward
    )
    feedforward_gain_part = lax.dynamic_slice_in_dim(feedforward_gain_full, col_start, col_width, 0)
    feedforward_grad = feedforward_full_grad.astype(jnp.bfloat16)
    activated_grad = times_transposed(feedforward_grad, down_matrix)
    down_weight_grad = transposed_times(activated, feedforward_grad)
    gate_grad = (
        activated_grad * up_rows * sigmoid_gate * (1.0 + gate * (1.0 - sigmoid_gate))
    ).astype(jnp.bfloat16)
    up_grad = (activated_grad * silu_gate).astype(jnp.bfloat16)
    hidden_part = times_transposed(gate_grad, gate_matrix) + times_transposed(up_grad, up_matrix)
    gate_weight_grad = transposed_times(hidden_low, gate_grad)
    up_weight_grad = transposed_times(hidden_low, up_grad)
    hidden_grad = lax.psum(hidden_part, "col") + upstream
    attention_full_grad, attention_gain_full = norm_back(
        hidden_grad, attention_out, attention_scale, gain_attention
    )
    attention_gain_part = lax.dynamic_slice_in_dim(attention_gain_full, col_start, col_width, 0)
    attention_grad = attention_full_grad.astype(jnp.bfloat16)
    residual_grad = lax.dynamic_slice_in_dim(hidden_grad, col_start, col_width, 1)
    context_grad = times_transposed(attention_grad, output_matrix).astype(jnp.bfloat16)
    output_weight_grad = transposed_times(context_low, attention_grad)
    query_rot_grad, key_rot_grad, value_grad = attend_back(
        query_rot, key_rot, value_low, context_grad, log_norm, segments, positions
    )
    value_grad = value_grad.astype(jnp.bfloat16)
    query_norm_grad = rotate(query_rot_grad, cosine_table, sine_table, -1.0)
    key_norm_grad = rotate(key_rot_grad, cosine_table, sine_table, -1.0)
    query_scaled = gain_query * query_norm_grad
    key_scaled = gain_key * key_norm_grad
    inner_sums = lax.psum(
        (jnp.sum(query_scaled * query_raw, axis=-1), jnp.sum(key_scaled * key_raw, axis=-1)), "col"
    )
    query_raw_grad = (
        query_scale * query_scaled
        - query_raw * query_scale * query_scale * query_scale * (inner_sums[0] / D)[:, None]
    ).astype(jnp.bfloat16)
    key_raw_grad = (
        key_scale * key_scaled
        - key_raw * key_scale * key_scale * key_scale * (inner_sums[1] / D)[:, None]
    ).astype(jnp.bfloat16)
    query_gain_part = jnp.sum(query_norm_grad * query_raw * query_scale, axis=0)
    key_gain_part = jnp.sum(key_norm_grad * key_raw * key_scale, axis=0)
    input_part = (
        times_transposed(query_raw_grad, query_matrix)
        + times_transposed(key_raw_grad, key_matrix)
        + times_transposed(value_grad, value_matrix)
    )
    query_weight_part = transposed_times(features, query_raw_grad)
    key_weight_part = transposed_times(features, key_raw_grad)
    value_weight_part = transposed_times(features, value_grad)
    input_grad = (
        lax.psum_scatter(
            input_part.astype(jnp.bfloat16), "col", scatter_dimension=1, tiled=True
        ).astype(jnp.float32)
        + residual_grad
    )
    weight_grads = (
        lax.psum_scatter(
            query_weight_part.astype(jnp.bfloat16), "row", scatter_dimension=0, tiled=True
        ).astype(jnp.float32),
        lax.psum_scatter(
            key_weight_part.astype(jnp.bfloat16), "row", scatter_dimension=0, tiled=True
        ).astype(jnp.float32),
        lax.psum_scatter(
            value_weight_part.astype(jnp.bfloat16), "row", scatter_dimension=0, tiled=True
        ).astype(jnp.float32),
        lax.psum_scatter(
            output_weight_grad.astype(jnp.bfloat16), "row", scatter_dimension=1, tiled=True
        ).astype(jnp.float32),
        lax.psum_scatter(
            gate_weight_grad.astype(jnp.bfloat16), "row", scatter_dimension=0, tiled=True
        ).astype(jnp.float32),
        lax.psum_scatter(
            up_weight_grad.astype(jnp.bfloat16), "row", scatter_dimension=0, tiled=True
        ).astype(jnp.float32),
        lax.psum_scatter(
            down_weight_grad.astype(jnp.bfloat16), "row", scatter_dimension=1, tiled=True
        ).astype(jnp.float32),
    )
    gain_totals = lax.psum(
        (
            spread_share(query_gain_part, col_start),
            spread_share(key_gain_part, col_start),
            spread_share(attention_gain_part, col_start),
            spread_share(feedforward_gain_part, col_start),
        ),
        ("row", "col"),
    )
    query_gain_grad = lax.dynamic_slice_in_dim(gain_totals[0], col_start, col_width, 0)
    key_gain_grad = lax.dynamic_slice_in_dim(gain_totals[1], col_start, col_width, 0)
    return (
        activations,
        input_grad,
        weight_grads[0],
        weight_grads[1],
        weight_grads[2],
        weight_grads[3],
        weight_grads[4],
        weight_grads[5],
        weight_grads[6],
        query_gain_grad,
        key_gain_grad,
        gain_totals[2],
        gain_totals[3],
    )


def solution(mesh):
    in_specs = (
        P("row", "col"),
        P("row", "col"),
        P("row", "col"),
        P("row", "col"),
        P("col", "row"),
        P("row", "col"),
        P("row", "col"),
        P("col", "row"),
        P("col"),
        P("col"),
        P(),
        P(),
        P("row"),
        P("row"),
        P("row", "col"),
    )
    out_specs = (
        P("row", "col"),
        P("row", "col"),
        P("row", "col"),
        P("row", "col"),
        P("row", "col"),
        P("col", "row"),
        P("row", "col"),
        P("row", "col"),
        P("col", "row"),
        P("col"),
        P("col"),
        P(),
        P(),
    )
    return jax.shard_map(body, mesh=mesh, in_specs=in_specs, out_specs=out_specs, check_vma=False)
```

profile of v0, /device:TPU:0, one launch (start us, length us, event | category | flops | bytes accessed | tf_op | source)
XLA Modules:
  0.0 2133.4 jit_solution(11342082336165431979)
XLA Ops:
  17.7 23.7 %all-gather.12.cloned.1.call-done = bf16[2048,512]{1,0:T(8,128)(2,1)} async-done(((bf16[256,512]{1,0:T(8,128)(2,1)}), bf16[2048,512]{1,0:T(8,128)(2,1)}) %all-gather.12.cloned.1.call-update) | async-done | bytes 2097168 | tf_op jit(solution)/shard_map/all_gather | solution.py:193
  41.5 71.2 %all-gather.10.cloned.1.call-done = bf16[1536,2048]{1,0:T(8,128)(2,1)} async-done(((bf16[1536,512]{1,0:T(8,128)(2,1)}), bf16[1536,2048]{1,0:T(8,128)(2,1)}) %all-gather.10.cloned.1.call-update) | async-done | bytes 6291472 | tf_op jit(solution)/shard_map/all_gather | solution.py:191
  119.0 24.5 %all-gather.14.cloned.1.call-done = bf16[2048,512]{1,0:T(8,128)(2,1)} async-done(((bf16[256,512]{1,0:T(8,128)(2,1)}), bf16[2048,512]{1,0:T(8,128)(2,1)}) %all-gather.14.cloned.1.call-update) | async-done | bytes 2097168 | tf_op jit(solution)/shard_map/all_gather | solution.py:194
  211.1 47.7 %while.29 = (s32[]{:T(128)}, bf16[3,512,512]{2,1,0:T(8,128)(2,1)}, f32[3,4,512]{2,1,0:T(4,128)}, s32[1536]{0:T(1024)S(1)}, s32[3,512]{1,0:T(4,128)S(1)}, /*index...) while((s32[]{:T(128)}, bf16[3,512,512]{2,1,0:T(8,128)(2,1)}, ...), condition=%wide.region_7.8_spmd.clone, body=%wide.region_4.7_spmd.sunk.clone | while | flops 1651506688 | bytes 54626440 | solution.py:100
  271.3 234.8 %all-reduce.7.cloned.1.call-done = f32[1536,2048]{1,0:T(8,128)} async-done(((f32[1536,2048]{1,0:T(8,128)}), f32[1536,2048]{1,0:T(8,128)}) %all-reduce.7.cloned.1.call-update) | async-done | bytes 12582928 | tf_op jit(solution)/shard_map/psum | solution.py:219
  524.9 64.8 %all-gather.20.cloned.1.call-done = bf16[2048,2048]{1,0:T(8,128)(2,1)} async-done(((bf16[256,2048]{1,0:T(8,128)(2,1)}), bf16[2048,2048]{1,0:T(8,128)(2,1)}) %all-gather.20.cloned.1.call-update) | async-done | bytes 8388624 | tf_op jit(solution)/shard_map/all_gather | solution.py:197
  608.7 63.2 %all-gather.22.cloned.1.call-done = bf16[2048,2048]{1,0:T(8,128)(2,1)} async-done(((bf16[256,2048]{1,0:T(8,128)(2,1)}), bf16[2048,2048]{1,0:T(8,128)(2,1)}) %all-gather.22.cloned.1.call-update) | async-done | bytes 8388624 | tf_op jit(solution)/shard_map/all_gather | solution.py:198
  671.9 23.5 %multiply_convert_fusion.3 = (bf16[1536,2048]{1,0:T(8,128)(2,1)}, f32[1536,2048]{1,0:T(8,128)}) fusion(f32[1536,2048]{1,0:T(8,128)} %fusion.36, bf16[1536,2048]{1,0:T(8,128)(2,1)} %get-tuple-element.317, bf16[2048,2048]{1,0:T(8,128)(2,1)} %all-gather.22.cloned.1.call-done), kind=kOutput, calls=%fused_computation.51 | convolution fusion | flops 12903776256 | bytes 46137344 | tf_op jit(solution)/shard_map/dot_general | solution.py:15
  695.5 59.0 %all-gather.24.cloned.1.call-done = bf16[2048,2048]{1,0:T(8,128)(2,1)} async-done(((bf16[2048,256]{1,0:T(8,128)(2,1)}), bf16[2048,2048]{1,0:T(8,128)(2,1)}) %all-gather.24.cloned.1.call-update) | async-done | bytes 8388624 | tf_op jit(solution)/shard_map/all_gather | solution.py:199
  774.4 236.7 %all-reduce.9.cloned.1.call-done = f32[1536,2048]{1,0:T(8,128)} async-done(((f32[1536,2048]{1,0:T(8,128)}), f32[1536,2048]{1,0:T(8,128)}) %all-reduce.9.cloned.1.call-update) | async-done | bytes 12582928 | tf_op jit(solution)/shard_map/psum | solution.py:231
  1016.5 66.3 %all-gather.26.cloned.1.call-done = bf16[1536,2048]{1,0:T(8,128)(2,1)} async-done(((bf16[1536,512]{1,0:T(8,128)(2,1)}), bf16[1536,2048]{1,0:T(8,128)(2,1)}) %all-gather.26.cloned.1.call-update) | async-done | bytes 6291472 | tf_op jit(solution)/shard_map/all_gather | solution.py:237
  1102.5 26.6 %multiply_convert_fusion.1 = (bf16[1536,2048]{1,0:T(8,128)(2,1)}, bf16[1536,2048]{1,0:T(8,128)(2,1)}) fusion(f32[1536,2048]{1,0:T(8,128)} %fusion.36, f32[1536,2048]{1,0:T(8,128)} %get-tuple-element.355, bf16[1536,2048]{1,0:T(8,128)(2,1)} %get-tuple-element.329, bf16[2048,2048]{1,0:T(8,128)(2,1)} %all-gather.24.cloned.1.call-done), kind=kOutput, calls=%fused_computation.48 | convolution fusion | flops 12925796352 | bytes 52428800 | tf_op jit(solution)/shard_map/dot_general | solution.py:19
  1148.4 20.7 convolution_add_fusion
  1173.6 234.9 %all-reduce.11.cloned.1.call-done = f32[1536,2048]{1,0:T(8,128)} async-done(((f32[1536,2048]{1,0:T(8,128)}), f32[1536,2048]{1,0:T(8,128)}) %all-reduce.11.cloned.1.call-update) | async-done | bytes 12582928 | tf_op jit(solution)/shard_map/psum | solution.py:252
  1436.2 127.1 %while.30 = (s32[]{:T(128)}, f32[1536,4,128]{0,2,1:T(8,128)}, f32[1536,4,128]{0,2,1:T(8,128)}, f32[3,512,512]{2,1,0:T(8,128)}, bf16[3,512,512]{1,2,0:T(8,128)(2,...) while((s32[]{:T(128)}, f32[1536,4,128]{0,2,1:T(8,128)}, ...), condition=%wide.region_17.18_spmd.clone.clone, body=%wide.region_15.17_spmd.clone.sunk.clone | while | flops 4062182912 | bytes 245442384 | solution.py:164
  1631.1 19.6 convolution_convert_fusion
  1670.6 20.3 convolution_convert_fusion.2
  1691.0 20.0 convolution_convert_fusion.1
  1758.0 41.1 %all-reduce = (f32[2048]{0:T(1024)S(1)}, f32[2048]{0:T(1024)S(1)}, f32[2048]{0:T(1024)}, f32[2048]{0:T(1024)}) all-reduce(f32[2048]{0:T(1024)S(1)} %dynamic_update_slice.23, f32[2048]{0:T(1024)S(1)} %dynamic_update_slice.24, f32[2048]{0:T(1024)S(1)} %dynamic-slice_dynamic-update-slice_fusion.1, ...), channel_id=1, replica_groups=mesh['row'=8,'col'=4] {'row','col'}, use_global_device_ids=true, to_apply=%region_31.32 | all-reduce | flops 8192 | bytes 65536 | tf_op jit(solution)/shard_map/psum | solution.py:319
  1806.8 25.9 %reduce-scatter.11.cloned.1.call-done = bf16[256,512]{0,1:T(8,128)(2,1)} async-done(((bf16[2048,512]{0,1:T(8,128)(2,1)}), bf16[256,512]{0,1:T(8,128)(2,1)}) %reduce-scatter.11.cloned.1.call-update) | async-done | bytes 262160 | tf_op jit(solution)/shard_map/reduce_scatter | solution.py:297
  1834.5 88.3 %reduce-scatter.19.cloned.1.call-done = bf16[256,2048]{1,0:T(8,128)(2,1)} async-done(((bf16[2048,2048]{1,0:T(8,128)(2,1)}), bf16[256,2048]{1,0:T(8,128)(2,1)}) %reduce-scatter.19.cloned.1.call-update) | async-done | bytes 1048592 | tf_op jit(solution)/shard_map/reduce_scatter | solution.py:309
  1925.6 87.4 %reduce-scatter.21.cloned.1.call-done = bf16[256,2048]{1,0:T(8,128)(2,1)} async-done(((bf16[2048,2048]{1,0:T(8,128)(2,1)}), bf16[256,2048]{1,0:T(8,128)(2,1)}) %reduce-scatter.21.cloned.1.call-update) | async-done | bytes 1048592 | tf_op jit(solution)/shard_map/reduce_scatter | solution.py:312
  2015.8 34.6 %reduce-scatter.15.cloned.1.call-done = bf16[256,512]{0,1:T(8,128)(2,1)} async-done(((bf16[2048,512]{0,1:T(8,128)(2,1)}), bf16[256,512]{0,1:T(8,128)(2,1)}) %reduce-scatter.15.cloned.1.call-update) | async-done | bytes 262160 | tf_op jit(solution)/shard_map/reduce_scatter | solution.py:303
  2052.3 69.5 %reduce-scatter.9.cloned.1.call-done = bf16[1536,512]{1,0:T(8,128)(2,1)} async-done(((bf16[1536,2048]{1,0:T(8,128)(2,1)}), bf16[1536,512]{1,0:T(8,128)(2,1)}) %reduce-scatter.9.cloned.1.call-update) | async-done | bytes 1572880 | tf_op jit(solution)/shard_map/reduce_scatter | solution.py:291
  (341 shorter events, 560.8 us)
Async XLA Ops:
  7.2 34.3 %all-gather.12.cloned.1.call-start = ((), (), s32[]{:S(2)}) async-start(), calls=%async_computation.9 | async-start | bytes 2359296 | tf_op jit(solution)/shard_map/all_gather | solution.py:193
  7.9 104.7 %all-gather.10.cloned.1.call-start = ((), (), s32[]{:S(2)}) async-start(), calls=%async_computation.8 | async-start | bytes 7864320 | tf_op jit(solution)/shard_map/all_gather | solution.py:191
  8.7 134.8 %all-gather.14.cloned.1.call-start = ((), (), s32[]{:S(2)}) async-start(), calls=%async_computation.10 | async-start | bytes 2359296 | tf_op jit(solution)/shard_map/all_gather | solution.py:194
  9.4 193.6 %all-gather.16.cloned.1.call-start = ((), (), s32[]{:S(2)}) async-start(), calls=%async_computation.11 | async-start | bytes 2359296 | tf_op jit(solution)/shard_map/all_gather | solution.py:195
  10.0 248.9 %all-gather.18.cloned.1.call-start = ((), (), s32[]{:S(2)}) async-start(), calls=%async_computation.12 | async-start | bytes 2359296 | tf_op jit(solution)/shard_map/all_gather | solution.py:196
  10.6 495.5 %all-reduce.7.cloned.1.call-start = ((), (), s32[]{:S(2)}) async-start(), calls=%async_computation.13 | async-start | bytes 25165824 | tf_op jit(solution)/shard_map/psum | solution.py:219
  269.0 320.8 %all-gather.20.cloned.1.call-start = ((), (), s32[]{:S(2)}) async-start(), calls=%async_computation.14 | async-start | bytes 9437184 | tf_op jit(solution)/shard_map/all_gather | solution.py:197
  269.7 402.2 %all-gather.22.cloned.1.call-start = ((), (), s32[]{:S(2)}) async-start(), calls=%async_computation.15 | async-start | bytes 9437184 | tf_op jit(solution)/shard_map/all_gather | solution.py:198
  270.5 484.0 %all-gather.24.cloned.1.call-start = ((), (), s32[]{:S(2)}) async-start(), calls=%async_computation.16 | async-start | bytes 9437184 | tf_op jit(solution)/shard_map/all_gather | solution.py:199
  271.2 241.1 %copy-start.42 = (f32[2048]{0:T(1024)S(1)}, f32[2048]{0:T(1024)}, u32[]{:S(2)}) copy-start(f32[2048]{0:T(1024)} %param.29) | copy-start | bytes 24580
  271.2 739.8 %all-reduce.9.cloned.1.call-start = ((), (), s32[]{:S(2)}) async-start(), calls=%async_computation.17 | async-start | bytes 25165824 | tf_op jit(solution)/shard_map/psum | solution.py:231
  773.4 309.4 %all-gather.26.cloned.1.call-start = ((), (), s32[]{:S(2)}) async-start(), calls=%async_computation.18 | async-start | bytes 7864320 | tf_op jit(solution)/shard_map/all_gather | solution.py:237
  774.2 308.6 %copy-start.44 = (f32[2048]{0:T(1024)S(1)}, f32[2048]{0:T(1024)}, u32[]{:S(2)}) copy-start(f32[2048]{0:T(1024)} %param.30) | copy-start | bytes 24580
  774.2 634.3 %all-reduce.11.cloned.1.call-start = ((), (), s32[]{:S(2)}) async-start(), calls=%async_computation.19 | async-start | bytes 25165824 | tf_op jit(solution)/shard_map/psum | solution.py:252
  1169.1 631.3 %reduce-scatter.13.cloned.1.call-start = ((), (), s32[]{:S(2)}) async-start(), calls=%async_computation.22 | async-start | bytes 2359296 | tf_op jit(solution)/shard_map/reduce_scatter | solution.py:300
  1170.5 238.1 %copy-start.39 = (f32[1536]{0:T(1024)S(1)}, f32[1536]{0:T(1024)}, u32[]{:S(2)}) copy-start(f32[1536]{0:T(1024)} %copy-done.38) | copy-start | bytes 18436
  1170.5 238.1 %copy-start.43 = (f32[2048]{0:T(1024)S(1)}, f32[2048]{0:T(1024)}, u32[]{:S(2)}) copy-start(f32[2048]{0:T(1024)} %param.29) | copy-start | bytes 24580
  1631.1 171.2 %reduce-scatter.23.cloned.1.call-start = ((), (), s32[]{:S(2)}) async-start(), calls=%async_computation.27 | async-start | bytes 9437184 | tf_op jit(solution)/shard_map/reduce_scatter | solution.py:315
  1650.8 154.2 %reduce-scatter.17.cloned.1.call-start = ((), (), s32[]{:S(2)}) async-start(), calls=%async_computation.24 | async-start | bytes 2359296 | tf_op jit(solution)/shard_map/reduce_scatter | solution.py:306
  1659.0 173.6 %reduce-scatter.11.cloned.1.call-start = ((), (), s32[]{:S(2)}) async-start(), calls=%async_computation.21 | async-start | bytes 2359296 | tf_op jit(solution)/shard_map/reduce_scatter | solution.py:297
  1670.6 252.3 %reduce-scatter.19.cloned.1.call-start = ((), (), s32[]{:S(2)}) async-start(), calls=%async_computation.25 | async-start | bytes 9437184 | tf_op jit(solution)/shard_map/reduce_scatter | solution.py:309
  1691.0 322.0 %reduce-scatter.21.cloned.1.call-start = ((), (), s32[]{:S(2)}) async-start(), calls=%async_computation.26 | async-start | bytes 9437184 | tf_op jit(solution)/shard_map/reduce_scatter | solution.py:312
  1711.0 339.4 %reduce-scatter.15.cloned.1.call-start = ((), (), s32[]{:S(2)}) async-start(), calls=%async_computation.23 | async-start | bytes 2359296 | tf_op jit(solution)/shard_map/reduce_scatter | solution.py:303
  1721.8 400.0 %reduce-scatter.9.cloned.1.call-start = ((), (), s32[]{:S(2)}) async-start(), calls=%async_computation.20 | async-start | bytes 7864320 | tf_op jit(solution)/shard_map/reduce_scatter | solution.py:291
  (62 other events, 442.5 us)
Sparse Core Ops, SparseCore 0:
  9.6 31.8 all-gather.11
  43.3 69.3 all-gather.9
  114.3 29.1 all-gather.13
  144.9 28.5 all-gather.15
  174.9 30.0 all-gather.17
  269.1 236.9 all-reduce.6
  507.7 82.0 all-gather.19
  591.4 80.5 all-gather.21
  673.5 80.9 all-gather.23
  773.6 237.4 all-reduce.8
  1012.9 69.8 all-gather.25
  1169.2 239.2 all-reduce.10
  1631.2 36.1 reduce-scatter.12
  1669.5 87.8 reduce-scatter.22
  1760.1 34.8 reduce-scatter.16
  1797.7 34.8 reduce-scatter.10
  1834.8 88.0 reduce-scatter.18
  1925.0 87.9 reduce-scatter.20
  2015.9 34.5 reduce-scatter.14
  2053.3 68.5 reduce-scatter.8
where the time goes:
time: 2140 us; the launch traced here: 2130 us
  waiting for transfers between devices  1390 us (65%)
  matrix products  384 us (18%)
  other arithmetic  160 us (7%)
  local copies, waits for them, and re-layouts  109 us (5%)
  blocking collectives  72.4 us (3%)
    psum x1, waiting for transfers between devices, body(): feedforward_out = lax.psum(feedforward_part, 'col')  237 us
    psum x1, waiting for transfers between devices, body(): hidden_grad = lax.psum(hidden_part, 'col') + upstream  235 us
    psum x1, waiting for transfers between devices, body(): attention_out = lax.psum(attention_part, 'col')  235 us
    dot_general x7, matrix products, times_transposed(): lax.dot_general(left, right, (((1,), (1,)), ((), ())), preferred_element_...  99.4 us
    dot_general x7, matrix products, times_plain(): return jnp.dot(left, right, preferred_element_type=jnp.float32)  94.4 us
    dot_general x7, matrix products, transposed_times(): lax.dot_general(left, right, (((0,), (0,)), ((), ())), preferred_element_...  90.8 us
    reduce_scatter x1, waiting for transfers between devices, body(): lax.psum_scatter(gate_weight_grad.astype(jnp.bfloat16), 'row', scatter_di...  88.3 us
    reduce_scatter x1, waiting for transfers between devices, body(): lax.psum_scatter(up_weight_grad.astype(jnp.bfloat16), 'row', scatter_dime...  87.4 us
  transfers between devices with their start and end apart: 20, of which 15 were waited for; matrix products, arithmetic and copies ran while one was open for 15% of the time, Pallas kernels for 0%

commit v1 on v0

--- a/solution.py
+++ b/solution.py
@@ -216,7 +216,8 @@
     context, log_norm = attend(query_rot, key_rot, value_low, segments, positions)
     context_low = context.astype(jnp.bfloat16)
     attention_part = times_plain(context_low, output_matrix)
-    attention_out = lax.psum(attention_part, "col")
+    parts = lax.all_gather(attention_part, "col", axis=0, tiled=False)
+    attention_out = parts.sum(axis=0)
     attention_scale = lax.rsqrt(
         jnp.mean(attention_out * attention_out, axis=-1, keepdims=True) + EPSILON
     )

time: 2140 us -> 2250 us (1.051)
  waiting for transfers between devices: 1390 us -> 1480 us
  other arithmetic: 160 us -> 186 us
    all_gather x0 -> x1, waiting for transfers between devices: none -> 432 us  [body(): parts = lax.all_gather(attention_part, 'col', axis=0, tiled=False)]
    psum x1 -> x0, waiting for transfers between devices: 235 us -> none  [body(): attention_out = lax.psum(attention_part, 'col')]
    reduce_scatter x1, waiting for transfers between devices: 88.3 us -> 10.7 us  [body(): lax.psum_scatter(gate_weight_grad.astype(jnp.bfloat16), 'row', scatter_di...]
    reduce_sum x0 -> x1, other arithmetic: none -> 24.1 us  [body(): attention_out = parts.sum(axis=0)]
    all_gather x1, waiting for transfers between devices: 64.8 us -> 41.2 us  [body(): lax.all_gather(weight_gate, 'row', axis=0, tiled=True)]
  transfers between devices with their start and end apart: 20 -> 20, of which waited for: 15 -> 15; matrix products, arithmetic and copies ran while one was open for 15% -> 24% of each run, Pallas kernels for 0% -> 0%
where the time goes in v1:
time: 2250 us; the launch traced here: 2240 us
  waiting for transfers between devices  1480 us (66%)
  matrix products  384 us (17%)
  other arithmetic  186 us (8%)
  local copies, waits for them, and re-layouts  107 us (5%)
  blocking collectives  73.2 us (3%)
    all_gather x1, waiting for transfers between devices, body(): parts = lax.all_gather(attention_part, 'col', axis=0, tiled=False)  432 us
    psum x1, waiting for transfers between devices, body(): feedforward_out = lax.psum(feedforward_part, 'col')  237 us
    psum x1, waiting for transfers between devices, body(): hidden_grad = lax.psum(hidden_part, 'col') + upstream  214 us
    dot_general x7, matrix products, times_transposed(): lax.dot_general(left, right, (((1,), (1,)), ((), ())), preferred_element_...  98.9 us
    dot_general x7, matrix products, times_plain(): return jnp.dot(left, right, preferred_element_type=jnp.float32)  94.7 us
    dot_general x7, matrix products, transposed_times(): lax.dot_general(left, right, (((0,), (0,)), ((), ())), preferred_element_...  90.8 us
    reduce_scatter x1, waiting for transfers between devices, body(): lax.psum_scatter(up_weight_grad.astype(jnp.bfloat16), 'row', scatter_dime...  87.4 us
    all_gather x1, waiting for transfers between devices, body(): features = lax.all_gather(tokens, 'col', axis=1, tiled=True)  71.2 us
  transfers between devices with their start and end apart: 20, of which 15 were waited for; matrix products, arithmetic and copies ran while one was open for 24% of the time, Pallas kernels for 0%

profile of v1, /device:TPU:0, one launch (start us, length us, event | category | flops | bytes accessed | tf_op | source)
XLA Modules:
  0.0 2242.8 jit_solution(16239942140528250872)
XLA Ops:
  17.7 23.8 %all-gather.14.cloned.1.call-done = bf16[2048,512]{1,0:T(8,128)(2,1)} async-done(((bf16[256,512]{1,0:T(8,128)(2,1)}), bf16[2048,512]{1,0:T(8,128)(2,1)}) %all-gather.14.cloned.1.call-update) | async-done | bytes 2097168 | tf_op jit(solution)/shard_map/all_gather | solution.py:193
  41.5 71.2 %all-gather.12.cloned.1.call-done = bf16[1536,2048]{1,0:T(8,128)(2,1)} async-done(((bf16[1536,512]{1,0:T(8,128)(2,1)}), bf16[1536,2048]{1,0:T(8,128)(2,1)}) %all-gather.12.cloned.1.call-update) | async-done | bytes 6291472 | tf_op jit(solution)/shard_map/all_gather | solution.py:191
  119.0 24.5 %all-gather.16.cloned.1.call-done = bf16[2048,512]{1,0:T(8,128)(2,1)} async-done(((bf16[256,512]{1,0:T(8,128)(2,1)}), bf16[2048,512]{1,0:T(8,128)(2,1)}) %all-gather.16.cloned.1.call-update) | async-done | bytes 2097168 | tf_op jit(solution)/shard_map/all_gather | solution.py:194
  211.2 48.1 %while.29 = (s32[]{:T(128)}, bf16[3,512,512]{2,1,0:T(8,128)(2,1)}, f32[3,4,512]{2,1,0:T(4,128)}, s32[1536]{0:T(1024)S(1)}, s32[3,512]{1,0:T(4,128)S(1)}, /*index...) while((s32[]{:T(128)}, bf16[3,512,512]{2,1,0:T(8,128)(2,1)}, ...), condition=%wide.region_7.8_spmd.clone, body=%wide.region_4.7_spmd.sunk.clone | while | flops 1651506688 | bytes 54626440 | solution.py:100
  271.6 432.4 %all-gather.30.cloned.1.call-done = f32[6144,2048]{1,0:T(8,128)} async-done(((f32[1536,2048]{1,0:T(8,128)}), f32[6144,2048]{1,0:T(8,128)}) %all-gather.30.cloned.1.call-update) | async-done | bytes 50331664 | tf_op jit(solution)/shard_map/all_gather | solution.py:219
  704.1 24.1 %reduce_sum.137 = f32[1536,2048]{1,0:T(8,128)} reduce(f32[4,1536,2048]{2,1,0:T(8,128)} %bitcast.194, f32[]{:T(128)} %constant.46.clone.1), dimensions={0}, to_apply=%region_8.9 | reduce | flops 9437184 | bytes 62914564 | tf_op jit(solution)/shard_map/reduce_sum | solution.py:220
  746.5 41.2 %all-gather.22.cloned.1.call-done = bf16[2048,2048]{1,0:T(8,128)(2,1)} async-done(((bf16[256,2048]{1,0:T(8,128)(2,1)}), bf16[2048,2048]{1,0:T(8,128)(2,1)}) %all-gather.22.cloned.1.call-update) | async-done | bytes 8388624 | tf_op jit(solution)/shard_map/all_gather | solution.py:197
  806.8 63.0 %all-gather.24.cloned.1.call-done = bf16[2048,2048]{1,0:T(8,128)(2,1)} async-done(((bf16[256,2048]{1,0:T(8,128)(2,1)}), bf16[2048,2048]{1,0:T(8,128)(2,1)}) %all-gather.24.cloned.1.call-update) | async-done | bytes 8388624 | tf_op jit(solution)/shard_map/all_gather | solution.py:198
  869.9 23.6 %multiply_convert_fusion.3 = (bf16[1536,2048]{1,0:T(8,128)(2,1)}, f32[1536,2048]{1,0:T(8,128)}) fusion(f32[1536,2048]{1,0:T(8,128)} %fusion.36, bf16[1536,2048]{1,0:T(8,128)(2,1)} %get-tuple-element.317, bf16[2048,2048]{1,0:T(8,128)(2,1)} %all-gather.24.cloned.1.call-done), kind=kOutput, calls=%fused_computation.51 | convolution fusion | flops 12903776256 | bytes 46137344 | tf_op jit(solution)/shard_map/dot_general | solution.py:15
  893.4 59.0 %all-gather.26.cloned.1.call-done = bf16[2048,2048]{1,0:T(8,128)(2,1)} async-done(((bf16[2048,256]{1,0:T(8,128)(2,1)}), bf16[2048,2048]{1,0:T(8,128)(2,1)}) %all-gather.26.cloned.1.call-update) | async-done | bytes 8388624 | tf_op jit(solution)/shard_map/all_gather | solution.py:199
  972.4 236.8 %all-reduce.6.cloned.1.call-done = f32[1536,2048]{1,0:T(8,128)} async-done(((f32[1536,2048]{1,0:T(8,128)}), f32[1536,2048]{1,0:T(8,128)}) %all-reduce.6.cloned.1.call-update) | async-done | bytes 12582928 | tf_op jit(solution)/shard_map/psum | solution.py:232
  1214.7 66.3 %all-gather.28.cloned.1.call-done = bf16[1536,2048]{1,0:T(8,128)(2,1)} async-done(((bf16[1536,512]{1,0:T(8,128)(2,1)}), bf16[1536,2048]{1,0:T(8,128)(2,1)}) %all-gather.28.cloned.1.call-update) | async-done | bytes 6291472 | tf_op jit(solution)/shard_map/all_gather | solution.py:238
  1300.8 26.4 %multiply_convert_fusion.1 = (bf16[1536,2048]{1,0:T(8,128)(2,1)}, bf16[1536,2048]{1,0:T(8,128)(2,1)}) fusion(f32[1536,2048]{1,0:T(8,128)} %fusion.36, f32[1536,2048]{1,0:T(8,128)} %get-tuple-element.355, bf16[1536,2048]{1,0:T(8,128)(2,1)} %get-tuple-element.329, bf16[2048,2048]{1,0:T(8,128)(2,1)} %all-gather.26.cloned.1.call-done), kind=kOutput, calls=%fused_computation.48 | convolution fusion | flops 12925796352 | bytes 52428800 | tf_op jit(solution)/shard_map/dot_general | solution.py:19
  1346.4 20.5 convolution_add_fusion
  1371.4 20.4 convolution_convert_fusion
  1391.9 214.5 %all-reduce.8.cloned.1.call-done = f32[1536,2048]{1,0:T(8,128)} async-done(((f32[1536,2048]{1,0:T(8,128)}), f32[1536,2048]{1,0:T(8,128)}) %all-reduce.8.cloned.1.call-update) | async-done | bytes 12582928 | tf_op jit(solution)/shard_map/psum | solution.py:253
  1635.1 127.7 %while.30 = (s32[]{:T(128)}, f32[1536,4,128]{0,2,1:T(8,128)}, f32[1536,4,128]{0,2,1:T(8,128)}, f32[3,512,512]{2,1,0:T(8,128)}, bf16[3,512,512]{1,2,0:T(8,128)(2,...) while((s32[]{:T(128)}, f32[1536,4,128]{0,2,1:T(8,128)}, ...), condition=%wide.region_17.18_spmd.clone.clone, body=%wide.region_15.17_spmd.clone.sunk.clone | while | flops 4062182912 | bytes 245442384 | solution.py:164
  1838.8 19.6 convolution_convert_fusion.2
  1858.4 19.9 convolution_convert_fusion.1
  1935.1 41.8 %all-reduce = (f32[2048]{0:T(1024)S(1)}, f32[2048]{0:T(1024)S(1)}, f32[2048]{0:T(1024)}, f32[2048]{0:T(1024)}) all-reduce(f32[2048]{0:T(1024)S(1)} %dynamic_update_slice.23, f32[2048]{0:T(1024)S(1)} %dynamic_update_slice.24, f32[2048]{0:T(1024)S(1)} %dynamic-slice_dynamic-update-slice_fusion.1, ...), channel_id=1, replica_groups=mesh['row'=8,'col'=4] {'row','col'}, use_global_device_ids=true, to_apply=%region_31.32 | all-reduce | flops 8192 | bytes 65536 | tf_op jit(solution)/shard_map/psum | solution.py:320
  1998.1 87.4 %reduce-scatter.21.cloned.1.call-done = bf16[256,2048]{1,0:T(8,128)(2,1)} async-done(((bf16[2048,2048]{1,0:T(8,128)(2,1)}), bf16[256,2048]{1,0:T(8,128)(2,1)}) %reduce-scatter.21.cloned.1.call-update) | async-done | bytes 1048592 | tf_op jit(solution)/shard_map/reduce_scatter | solution.py:313
  2088.3 34.4 %reduce-scatter.11.cloned.1.call-done = bf16[256,512]{0,1:T(8,128)(2,1)} async-done(((bf16[2048,512]{0,1:T(8,128)(2,1)}), bf16[256,512]{0,1:T(8,128)(2,1)}) %reduce-scatter.11.cloned.1.call-update) | async-done | bytes 262160 | tf_op jit(solution)/shard_map/reduce_scatter | solution.py:298
  2124.5 35.2 %reduce-scatter.15.cloned.1.call-done = bf16[256,512]{0,1:T(8,128)(2,1)} async-done(((bf16[2048,512]{0,1:T(8,128)(2,1)}), bf16[256,512]{0,1:T(8,128)(2,1)}) %reduce-scatter.15.cloned.1.call-update) | async-done | bytes 262160 | tf_op jit(solution)/shard_map/reduce_scatter | solution.py:304
  2161.6 69.7 %reduce-scatter.9.cloned.1.call-done = bf16[1536,512]{1,0:T(8,128)(2,1)} async-done(((bf16[1536,2048]{1,0:T(8,128)(2,1)}), bf16[1536,512]{1,0:T(8,128)(2,1)}) %reduce-scatter.9.cloned.1.call-update) | async-done | bytes 1572880 | tf_op jit(solution)/shard_map/reduce_scatter | solution.py:292
  (340 shorter events, 571.1 us)
Async XLA Ops:
  7.2 34.3 %all-gather.14.cloned.1.call-start = ((), (), s32[]{:S(2)}) async-start(), calls=%async_computation.9 | async-start | bytes 2359296 | tf_op jit(solution)/shard_map/all_gather | solution.py:193
  7.9 104.7 %all-gather.12.cloned.1.call-start = ((), (), s32[]{:S(2)}) async-start(), calls=%async_computation.8 | async-start | bytes 7864320 | tf_op jit(solution)/shard_map/all_gather | solution.py:191
  8.7 134.8 %all-gather.16.cloned.1.call-start = ((), (), s32[]{:S(2)}) async-start(), calls=%async_computation.10 | async-start | bytes 2359296 | tf_op jit(solution)/shard_map/all_gather | solution.py:194
  9.4 193.7 %all-gather.18.cloned.1.call-start = ((), (), s32[]{:S(2)}) async-start(), calls=%async_computation.11 | async-start | bytes 2359296 | tf_op jit(solution)/shard_map/all_gather | solution.py:195
  10.0 249.3 %all-gather.20.cloned.1.call-start = ((), (), s32[]{:S(2)}) async-start(), calls=%async_computation.12 | async-start | bytes 2359296 | tf_op jit(solution)/shard_map/all_gather | solution.py:196
  10.6 693.5 %all-gather.30.cloned.1.call-start = ((), (), s32[]{:S(2)}) async-start(), calls=%async_computation.27 | async-start | bytes 62914560 | tf_op jit(solution)/shard_map/all_gather | solution.py:219
  118.9 49.5 %copy-start.11 = (f32[1536,512]{0,1:T(8,128)}, f32[1536,512]{0,1:T(8,128)S(1)}, u32[]{:S(2)}) copy-start(f32[1536,512]{0,1:T(8,128)S(1)} %get-tuple-element.351) | copy-start | bytes 9437188
  269.3 518.4 %all-gather.22.cloned.1.call-start = ((), (), s32[]{:S(2)}) async-start(), calls=%async_computation.13 | async-start | bytes 9437184 | tf_op jit(solution)/shard_map/all_gather | solution.py:197
  270.1 599.8 %all-gather.24.cloned.1.call-start = ((), (), s32[]{:S(2)}) async-start(), calls=%async_computation.14 | async-start | bytes 9437184 | tf_op jit(solution)/shard_map/all_gather | solution.py:198
  270.8 681.6 %all-gather.26.cloned.1.call-start = ((), (), s32[]{:S(2)}) async-start(), calls=%async_computation.15 | async-start | bytes 9437184 | tf_op jit(solution)/shard_map/all_gather | solution.py:199
  271.6 937.7 %all-reduce.6.cloned.1.call-start = ((), (), s32[]{:S(2)}) async-start(), calls=%async_computation.16 | async-start | bytes 25165824 | tf_op jit(solution)/shard_map/psum | solution.py:232
  971.6 309.4 %all-gather.28.cloned.1.call-start = ((), (), s32[]{:S(2)}) async-start(), calls=%async_computation.17 | async-start | bytes 7864320 | tf_op jit(solution)/shard_map/all_gather | solution.py:238
  972.4 308.7 %copy-start.43 = (f32[2048]{0:T(1024)S(1)}, f32[2048]{0:T(1024)}, u32[]{:S(2)}) copy-start(f32[2048]{0:T(1024)} %param.30) | copy-start | bytes 24580
  972.4 634.0 %all-reduce.8.cloned.1.call-start = ((), (), s32[]{:S(2)}) async-start(), calls=%async_computation.18 | async-start | bytes 25165824 | tf_op jit(solution)/shard_map/psum | solution.py:253
  1366.9 611.3 %reduce-scatter.23.cloned.1.call-start = ((), (), s32[]{:S(2)}) async-start(), calls=%async_computation.26 | async-start | bytes 9437184 | tf_op jit(solution)/shard_map/reduce_scatter | solution.py:316
  1391.8 214.6 %copy-start.38 = (f32[1536]{0:T(1024)S(1)}, f32[1536]{0:T(1024)}, u32[]{:S(2)}) copy-start(f32[1536]{0:T(1024)} %copy-done.37) | copy-start | bytes 18436
  1391.8 214.6 %copy-start.42 = (f32[2048]{0:T(1024)S(1)}, f32[2048]{0:T(1024)}, u32[]{:S(2)}) copy-start(f32[2048]{0:T(1024)} %param.29) | copy-start | bytes 24580
  1391.9 589.1 %reduce-scatter.13.cloned.1.call-start = ((), (), s32[]{:S(2)}) async-start(), calls=%async_computation.21 | async-start | bytes 2359296 | tf_op jit(solution)/shard_map/reduce_scatter | solution.py:301
  1830.6 152.2 %reduce-scatter.17.cloned.1.call-start = ((), (), s32[]{:S(2)}) async-start(), calls=%async_computation.23 | async-start | bytes 2359296 | tf_op jit(solution)/shard_map/reduce_scatter | solution.py:307
  1838.7 156.6 %reduce-scatter.19.cloned.1.call-start = ((), (), s32[]{:S(2)}) async-start(), calls=%async_computation.24 | async-start | bytes 9437184 | tf_op jit(solution)/shard_map/reduce_scatter | solution.py:310
  1858.4 227.1 %reduce-scatter.21.cloned.1.call-start = ((), (), s32[]{:S(2)}) async-start(), calls=%async_computation.25 | async-start | bytes 9437184 | tf_op jit(solution)/shard_map/reduce_scatter | solution.py:313
  1878.3 244.3 %reduce-scatter.11.cloned.1.call-start = ((), (), s32[]{:S(2)}) async-start(), calls=%async_computation.20 | async-start | bytes 2359296 | tf_op jit(solution)/shard_map/reduce_scatter | solution.py:298
  1890.1 269.7 %reduce-scatter.15.cloned.1.call-start = ((), (), s32[]{:S(2)}) async-start(), calls=%async_computation.22 | async-start | bytes 2359296 | tf_op jit(solution)/shard_map/reduce_scatter | solution.py:304
  1899.0 332.3 %reduce-scatter.9.cloned.1.call-start = ((), (), s32[]{:S(2)}) async-start(), calls=%async_computation.19 | async-start | bytes 7864320 | tf_op jit(solution)/shard_map/reduce_scatter | solution.py:292
  (61 other events, 404.6 us)
Sparse Core Ops, SparseCore 0:
  9.6 31.8 all-gather.13
  43.3 69.2 all-gather.11
  114.3 29.1 all-gather.15
  144.9 28.5 all-gather.17
  174.9 29.9 all-gather.19
  269.5 434.5 all-gather.29
  705.7 82.0 all-gather.21
  789.3 80.5 all-gather.23
  871.5 80.9 all-gather.25
  971.7 237.4 all-reduce.5
  1211.1 69.8 all-gather.27
  1367.0 239.2 all-reduce.7
  1608.7 89.5 reduce-scatter.22
  1830.7 35.9 reduce-scatter.12
  1869.4 34.6 reduce-scatter.16
  1906.2 89.0 reduce-scatter.18
  1997.4 88.0 reduce-scatter.20
  2088.2 34.3 reduce-scatter.10
  2124.9 34.7 reduce-scatter.14
  2162.6 68.6 reduce-scatter.8
